TPU v7x, 32 devices: a whole 2x2x4 slice. The times are simulated.
32 devices in a mesh: lat: 4 (over z), lon: 4 (over y, x), lev: 2 (over core).
Axes of the slice: x: 2, y: 2, z: 4, core: 2. Of those that a mesh axis runs over, the one named last changes fastest.
Arguments:
- pressure: float32 [16, 256, 128, 128], P('lat', 'lon', 'lev'), may hold values from 0.2 to 1.8
- earlier: float32 [16, 256, 128, 128], P('lat', 'lon', 'lev'), may hold values from 0.2 to 1.8
- speed_square: float32 [16, 256, 128, 128], P('lat', 'lon', 'lev'), may hold values from 0.05 to 0.3
Outputs:
- pressure_end: float32 [16, 256, 128, 128], P('lat', 'lon', 'lev')
All inputs are finite; a program needn't handle non-finite values.
Results may differ from a plain program's by a relative error of at most 0.00002.
Values sent between devices are 32-bit elements.
A program may use at most 320 MiB of HBM per device.

v0:
```python
import jax
import jax.numpy as jnp
from jax import lax
from jax.sharding import PartitionSpec as P

STEPS = 4


def extended(block, sides, width):
    for axis, dim in sides:
        count = lax.axis_size(axis)
        forward = [(i, i + 1) for i in range(count - 1)]
        backward = [(target, source) for source, target in forward]
        low = lax.ppermute(
            lax.slice_in_dim(block, block.shape[dim] - width, None, axis=dim), axis, forward
        )
        high = lax.ppermute(lax.slice_in_dim(block, 0, width, axis=dim), axis, backward)
        block = jnp.concatenate([low, block, high], axis=dim)
    return block


def inner_cells(values, dims):
    for dim in dims:
        values = lax.slice_in_dim(values, 1, values.shape[dim] - 1, axis=dim)
    return values


def side_cells(values, dim, start, dims):
    others = [other for other in dims if other != dim]
    values = inner_cells(values, others)
    return lax.slice_in_dim(values, start, start + values.shape[dim] - 2, axis=dim)


def advance(padded, before, speed_square):
    middle = inner_cells(padded, (0, 1, 2))
    lower = [side_cells(padded, dim, 0, (0, 1, 2)) for dim in (0, 1, 2)]
    upper = [side_cells(padded, dim, 2, (0, 1, 2)) for dim in (0, 1, 2)]
    spread = lower[0] + upper[0] + lower[1] + upper[1] + lower[2] + upper[2] - 6.0 * middle
    return 2.0 * middle - before + speed_square * spread


def shards(pressure, earlier, speed_square):
    for step in range(STEPS):
        padded = extended(pressure, (("lat", 0), ("lon", 1), ("lev", 2)), 1)
        later = advance(padded, earlier, speed_square)
        earlier, pressure = (pressure, later)
    return pressure


def solution(mesh):
    return jax.shard_map(
        shards,
        mesh=mesh,
        in_specs=(
            P("lat", "lon", "lev", None),
            P("lat", "lon", "lev", None),
            P("lat", "lon", "lev", None),
        ),
        out_specs=P("lat", "lon", "lev", None),
        check_vma=False,
    )
```

profile of v0, /device:TPU:0, one launch (start us, length us, event | category | flops | bytes accessed | tf_op | source)
XLA Modules:
  0.0 410.5 jit_solution(15187204011936680499)
XLA Ops:
  0.0 4.1 %fusion.36 = (f32[1,64,64,128]{3,2,1,0:T(8,128)}, f32[1,64,64,128]{3,2,1,0:T(8,128)S(1)}) fusion(f32[4,64,64,128]{3,2,1,0:T(8,128)} %param.3), kind=kLoop, calls=%fused_computation.130 | loop fusion | bytes 8388608 | tf_op jit(solution)/shard_map/slice | solution.py:17
  4.1 5.2 %collective-permute-start = (f32[1,64,64,128]{3,2,1,0:T(8,128)S(1)}, f32[1,64,64,128]{3,2,1,0:T(8,128)S(1)}, u32[]{:S(2)}, u32[]{:S(2)}) collective-permute-start(f32[1,64,64,128]{3,2,1,0:T(8,128)S(1)} %get-tuple-element.28), channel_id=1, source_target_pairs={{0,8},{8,16},{16,24},{1,9},{9,17},{17,25},{2,10},{10,18},{18,26},{... | collective-permute-start | bytes 6291464 | tf_op jit(solution)/shard_map/ppermute | solution.py:14
  9.4 1.3 collective-permute-start.1
  10.7 43.4 %collective-permute-done = f32[1,64,64,128]{3,2,1,0:T(8,128)S(1)} collective-permute-done((f32[1,64,64,128]{3,2,1,0:T(8,128)S(1)}, f32[1,64,64,128]{3,2,1,0:T(8,128)S(1)}, u32[]{:S(2)}, u32[]{:S(2)}) %collective-permute-start) | collective-permute-done | bytes 2097184 | tf_op jit(solution)/shard_map/ppermute | solution.py:14
  54.1 1.3 copy-done.8
  55.4 0.2 constant_dynamic-update-slice_fusion.2
  55.6 1.7 constant_dynamic-update-slice_fusion.1
  57.3 1.4 collective-permute-done.1
  58.7 1.7 constant_dynamic-update-slice_fusion
  60.4 3.4 collective-permute-start.2
  63.9 1.3 collective-permute-start.3
  65.2 1.9 collective-permute-done.2
  67.0 6.1 %collective-permute-done.3 = f32[6,1,64,128]{3,2,1,0:T(8,128)S(1)} collective-permute-done((f32[6,1,64,128]{3,2,1,0:T(8,128)S(1)}, f32[6,1,64,128]{3,2,1,0:T(8,128)S(1)}, u32[]{:S(2)}, u32[]{:S(2)}) %collective-permute-start.3) | collective-permute-done | bytes 196640 | tf_op jit(solution)/shard_map/ppermute | solution.py:17
  73.1 0.3 pad_maximum_fusion.81
  73.4 1.3 collective-permute-start.5
  74.7 3.1 collective-permute-start.4
  77.8 0.2 copy.21
  78.0 0.8 collective-permute-done.4
  79.1 27.5 %fusion.27 = f32[4,64,64,128]{3,2,1,0:T(8,128)S(1)} fusion(f32[4,64,64,128]{3,2,1,0:T(8,128)} %param.5, f32[6,66,1,128]{3,2,1,0:T(1,128)S(1)} %copy.21, f32[6,1,64,128]{3,2,1,0:T(8,128)S(1)} %collective-permute-done.3, f32[6,64,64,128]{3,2,1,0:T(8,128)} %copy-done.4, f32[6,1,64,128]{3,2,1,0:T(8,128)S(1)} %collective-permute-done.2, ...), kind=kLoop, calls=%fused_computation.82 | loop fusion | flops 44040192 | bytes 51130368 | tf_op jit(solution)/shard_map/add | solution.py:39
  106.6 0.5 fusion.35
  107.2 3.6 collective-permute-start.6
  110.7 1.3 collective-permute-start.7
  112.0 44.0 %collective-permute-done.6 = f32[1,64,64,128]{3,2,1,0:T(8,128)S(1)} collective-permute-done((f32[1,64,64,128]{3,2,1,0:T(8,128)S(1)}, f32[1,64,64,128]{3,2,1,0:T(8,128)S(1)}, u32[]{:S(2)}, u32[]{:S(2)}) %collective-permute-start.6) | collective-permute-done | bytes 2097184 | tf_op jit(solution)/shard_map/ppermute | solution.py:14
  156.0 4.2 %collective-permute-done.7 = f32[1,64,64,128]{3,2,1,0:T(8,128)S(1)} collective-permute-done((f32[1,64,64,128]{3,2,1,0:T(8,128)S(1)}, f32[1,64,64,128]{3,2,1,0:T(8,128)S(1)}, u32[]{:S(2)}, u32[]{:S(2)}) %collective-permute-start.7) | collective-permute-done | bytes 2097184 | tf_op jit(solution)/shard_map/ppermute | solution.py:17
  160.3 3.4 collective-permute-start.8
  163.7 1.3 collective-permute-start.9
  165.0 2.2 collective-permute-done.8
  167.2 5.0 %collective-permute-done.9 = f32[6,1,64,128]{3,2,1,0:T(8,128)S(1)} collective-permute-done((f32[6,1,64,128]{3,2,1,0:T(8,128)S(1)}, f32[6,1,64,128]{3,2,1,0:T(8,128)S(1)}, u32[]{:S(2)}, u32[]{:S(2)}) %collective-permute-start.9) | collective-permute-done | bytes 196640 | tf_op jit(solution)/shard_map/ppermute | solution.py:17
  172.2 0.3 pad_maximum_fusion.78
  172.5 1.3 collective-permute-start.11
  173.9 3.2 collective-permute-start.10
  177.1 0.2 copy.25
  177.3 0.7 collective-permute-done.10
  178.2 28.9 %fusion.19 = f32[4,64,64,128]{3,2,1,0:T(8,128)} fusion(f32[4,64,64,128]{3,2,1,0:T(8,128)} %param.5, f32[6,66,1,128]{3,2,1,0:T(1,128)S(1)} %copy.25, f32[6,1,64,128]{3,2,1,0:T(8,128)S(1)} %collective-permute-done.9, f32[6,1,64,128]{3,2,1,0:T(8,128)S(1)} %collective-permute-done.8, f32[1,64,64,128]{3,2,1,0:T(8,128)} %copy-done.7, ...), kind=kLoop, calls=%fused_computation.56 | loop fusion | flops 60817408 | bytes 38547456 | tf_op jit(solution)/shard_map/add | solution.py:39
  207.1 2.7 fusion.34
  209.8 3.7 collective-permute-start.12
  213.6 1.3 collective-permute-start.13
  214.9 44.0 %collective-permute-done.12 = f32[1,64,64,128]{3,2,1,0:T(8,128)S(1)} collective-permute-done((f32[1,64,64,128]{3,2,1,0:T(8,128)S(1)}, f32[1,64,64,128]{3,2,1,0:T(8,128)S(1)}, u32[]{:S(2)}, u32[]{:S(2)}) %collective-permute-start.12) | collective-permute-done | bytes 2097184 | tf_op jit(solution)/shard_map/ppermute | solution.py:14
  258.9 4.2 %collective-permute-done.13 = f32[1,64,64,128]{3,2,1,0:T(8,128)S(1)} collective-permute-done((f32[1,64,64,128]{3,2,1,0:T(8,128)S(1)}, f32[1,64,64,128]{3,2,1,0:T(8,128)S(1)}, u32[]{:S(2)}, u32[]{:S(2)}) %collective-permute-start.13) | collective-permute-done | bytes 2097184 | tf_op jit(solution)/shard_map/ppermute | solution.py:17
  263.1 2.3 collective-permute-start.14
  265.4 1.3 collective-permute-start.15
  266.7 2.2 collective-permute-done.14
  268.9 5.0 %collective-permute-done.15 = f32[6,1,64,128]{3,2,1,0:T(8,128)S(1)} collective-permute-done((f32[6,1,64,128]{3,2,1,0:T(8,128)S(1)}, f32[6,1,64,128]{3,2,1,0:T(8,128)S(1)}, u32[]{:S(2)}, u32[]{:S(2)}) %collective-permute-start.15) | collective-permute-done | bytes 196640 | tf_op jit(solution)/shard_map/ppermute | solution.py:17
  273.9 0.3 pad_maximum_fusion.73
  274.2 1.3 collective-permute-start.17
  275.6 3.1 collective-permute-start.16
  278.6 0.2 copy.29
  278.8 0.8 collective-permute-done.16
  279.9 28.9 %fusion.11 = f32[4,64,64,128]{3,2,1,0:T(8,128)} fusion(f32[4,64,64,128]{3,2,1,0:T(8,128)} %param.5, f32[6,66,1,128]{3,2,1,0:T(1,128)S(1)} %copy.29, f32[6,1,64,128]{3,2,1,0:T(8,128)S(1)} %collective-permute-done.15, f32[6,1,64,128]{3,2,1,0:T(8,128)S(1)} %collective-permute-done.14, f32[1,64,64,128]{3,2,1,0:T(8,128)} %copy-done.6, ...), kind=kLoop, calls=%fused_computation.30 | loop fusion | flops 60817408 | bytes 38547456 | tf_op jit(solution)/shard_map/add | solution.py:39
  308.8 2.7 fusion.33
  311.5 3.6 collective-permute-start.18
  315.1 1.3 collective-permute-start.19
  316.4 44.0 %collective-permute-done.18 = f32[1,64,64,128]{3,2,1,0:T(8,128)S(1)} collective-permute-done((f32[1,64,64,128]{3,2,1,0:T(8,128)S(1)}, f32[1,64,64,128]{3,2,1,0:T(8,128)S(1)}, u32[]{:S(2)}, u32[]{:S(2)}) %collective-permute-start.18) | collective-permute-done | bytes 2097184 | tf_op jit(solution)/shard_map/ppermute | solution.py:14
  360.4 4.2 %collective-permute-done.19 = f32[1,64,64,128]{3,2,1,0:T(8,128)S(1)} collective-permute-done((f32[1,64,64,128]{3,2,1,0:T(8,128)S(1)}, f32[1,64,64,128]{3,2,1,0:T(8,128)S(1)}, u32[]{:S(2)}, u32[]{:S(2)}) %collective-permute-start.19) | collective-permute-done | bytes 2097184 | tf_op jit(solution)/shard_map/ppermute | solution.py:17
  364.7 2.3 collective-permute-start.20
  366.9 1.3 collective-permute-start.21
  368.2 2.2 collective-permute-done.20
  370.5 5.0 %collective-permute-done.21 = f32[6,1,64,128]{3,2,1,0:T(8,128)S(1)} collective-permute-done((f32[6,1,64,128]{3,2,1,0:T(8,128)S(1)}, f32[6,1,64,128]{3,2,1,0:T(8,128)S(1)}, u32[]{:S(2)}, u32[]{:S(2)}) %collective-permute-start.21) | collective-permute-done | bytes 196640 | tf_op jit(solution)/shard_map/ppermute | solution.py:17
  375.4 0.3 pad_maximum_fusion.68
  375.8 1.3 collective-permute-start.23
  377.1 3.3 collective-permute-start.22
  380.4 0.2 copy.33
  380.6 0.6 collective-permute-done.22
  381.4 28.9 %fusion.3 = f32[4,64,64,128]{3,2,1,0:T(8,128)} fusion(f32[4,64,64,128]{3,2,1,0:T(8,128)} %param.5, f32[6,66,1,128]{3,2,1,0:T(1,128)S(1)} %copy.33, f32[6,1,64,128]{3,2,1,0:T(8,128)S(1)} %collective-permute-done.21, f32[6,1,64,128]{3,2,1,0:T(8,128)S(1)} %collective-permute-done.20, f32[1,64,64,128]{3,2,1,0:T(8,128)} %copy-done.5, ...), kind=kLoop, calls=%fused_computation.4 | loop fusion | flops 60817408 | bytes 38547456 | tf_op jit(solution)/shard_map/add | solution.py:39
  (37 shorter events, 1.1 us)
Async XLA Ops:
  0.0 55.6 %copy-start.3 = (f32[4,64,64,128]{3,2,1,0:T(8,128)S(1)}, f32[4,64,64,128]{3,2,1,0:T(8,128)}, u32[]{:S(2)}) copy-start(f32[4,64,64,128]{3,2,1,0:T(8,128)} %param.3) | copy-start | bytes 25165828
  4.1 50.0 %collective-permute-start = (f32[1,64,64,128]{3,2,1,0:T(8,128)S(1)}, f32[1,64,64,128]{3,2,1,0:T(8,128)S(1)}, u32[]{:S(2)}, u32[]{:S(2)}) collective-permute-start(f32[1,64,64,128]{3,2,1,0:T(8,128)S(1)} %get-tuple-element.28), channel_id=1, source_target_pairs={{0,8},{8,16},{16,24},{1,9},{9,17},{17,25},{2,10},{10,18},{18,26},{... | collective-permute-start | bytes 6291464 | tf_op jit(solution)/shard_map/ppermute | solution.py:14
  9.4 49.3 %collective-permute-start.1 = (f32[1,64,64,128]{3,2,1,0:T(8,128)}, f32[1,64,64,128]{3,2,1,0:T(8,128)}, u32[]{:S(2)}, u32[]{:S(2)}) collective-permute-start(f32[1,64,64,128]{3,2,1,0:T(8,128)} %get-tuple-element.27), channel_id=1, source_target_pairs={{8,0},{16,8},{24,16},{9,1},{17,9},{25,17},{10,2},{18,10},{26,18},{... | collective-permute-start | bytes 6291464 | tf_op jit(solution)/shard_map/ppermute | solution.py:17
  54.1 1.3 copy-start.8
  60.4 18.5 %copy-start.4 = (f32[6,64,64,128]{3,2,1,0:T(8,128)}, f32[6,64,64,128]{3,2,1,0:T(8,128)S(1)}, u32[]{:S(2)}) copy-start(f32[6,64,64,128]{3,2,1,0:T(8,128)S(1)} %constant_dynamic-update-slice_fusion) | copy-start | bytes 37748740
  60.4 6.6 %collective-permute-start.2 = (f32[6,1,64,128]{3,2,1,0:T(8,128)S(1)}, f32[6,1,64,128]{3,2,1,0:T(8,128)S(1)}, u32[]{:S(2)}, u32[]{:S(2)}) collective-permute-start(f32[6,1,64,128]{3,2,1,0:T(8,128)S(1)} %get-tuple-element.19), channel_id=1, source_target_pairs={{0,2},{2,4},{4,6},{1,3},{3,5},{5,7},{8,10},{10,12},{12,14},{9,11},... | collective-permute-start | bytes 589832 | tf_op jit(solution)/shard_map/ppermute | solution.py:14
  63.9 9.2 %collective-permute-start.3 = (f32[6,1,64,128]{3,2,1,0:T(8,128)S(1)}, f32[6,1,64,128]{3,2,1,0:T(8,128)S(1)}, u32[]{:S(2)}, u32[]{:S(2)}) collective-permute-start(f32[6,1,64,128]{3,2,1,0:T(8,128)S(1)} %get-tuple-element.20), channel_id=1, source_target_pairs={{2,0},{4,2},{6,4},{3,1},{5,3},{7,5},{10,8},{12,10},{14,12},{11,9},... | collective-permute-start | bytes 589832 | tf_op jit(solution)/shard_map/ppermute | solution.py:17
  73.4 4.4 %collective-permute-start.5 = (f32[6,66,1,128]{3,1,2,0:T(8,128)S(1)}, f32[6,66,1,128]{3,1,2,0:T(8,128)S(1)}, u32[]{:S(2)}, u32[]{:S(2)}) collective-permute-start(f32[6,66,1,128]{3,1,2,0:T(8,128)S(1)} %copy.20), channel_id=1, source_target_pairs={{1,0},{3,2},{5,4},{7,6},{9,8},{11,10},{13,12},{15,14},{17,16},{19,... | collective-permute-start | bytes 608264 | tf_op jit(solution)/shard_map/ppermute | solution.py:17
  74.7 4.1 %collective-permute-start.4 = (f32[6,66,1,128]{3,1,2,0:T(8,128)S(1)}, f32[6,66,1,128]{3,1,2,0:T(8,128)S(1)}, u32[]{:S(2)}, u32[]{:S(2)}) collective-permute-start(f32[6,66,1,128]{3,1,2,0:T(8,128)S(1)} %copy.18), channel_id=1, source_target_pairs={{0,1},{2,3},{4,5},{6,7},{8,9},{10,11},{12,13},{14,15},{16,17},{18,... | collective-permute-start | bytes 608264 | tf_op jit(solution)/shard_map/ppermute | solution.py:14
  106.6 65.6 %copy-start = (f32[4,64,64,128]{3,2,1,0:T(8,128)}, f32[4,64,64,128]{3,2,1,0:T(8,128)S(1)}, u32[]{:S(2)}) copy-start(f32[4,64,64,128]{3,2,1,0:T(8,128)S(1)} %fusion.27) | copy-start | bytes 25165828
  107.2 48.8 %collective-permute-start.6 = (f32[1,64,64,128]{3,2,1,0:T(8,128)S(1)}, f32[1,64,64,128]{3,2,1,0:T(8,128)S(1)}, u32[]{:S(2)}, u32[]{:S(2)}) collective-permute-start(f32[1,64,64,128]{3,2,1,0:T(8,128)S(1)} %get-tuple-element.25), channel_id=1, source_target_pairs={{0,8},{8,16},{16,24},{1,9},{9,17},{17,25},{2,10},{10,18},{18,26},{... | collective-permute-start | bytes 6291464 | tf_op jit(solution)/shard_map/ppermute | solution.py:14
  110.7 49.5 %collective-permute-start.7 = (f32[1,64,64,128]{3,2,1,0:T(8,128)S(1)}, f32[1,64,64,128]{3,2,1,0:T(8,128)S(1)}, u32[]{:S(2)}, u32[]{:S(2)}) collective-permute-start(f32[1,64,64,128]{3,2,1,0:T(8,128)S(1)} %get-tuple-element.26), channel_id=1, source_target_pairs={{8,0},{16,8},{24,16},{9,1},{17,9},{25,17},{10,2},{18,10},{26,18},{... | collective-permute-start | bytes 6291464 | tf_op jit(solution)/shard_map/ppermute | solution.py:17
  160.2 12.2 %copy-start.7 = (f32[1,64,64,128]{3,2,1,0:T(8,128)}, f32[1,64,64,128]{3,2,1,0:T(8,128)S(1)}, u32[]{:S(2)}) copy-start(f32[1,64,64,128]{3,2,1,0:T(8,128)S(1)} %collective-permute-done.7) | copy-start | bytes 6291460
  160.3 7.0 %collective-permute-start.8 = (f32[6,1,64,128]{3,2,1,0:T(8,128)S(1)}, f32[6,1,64,128]{3,2,1,0:T(8,128)S(1)}, u32[]{:S(2)}, u32[]{:S(2)}) collective-permute-start(f32[6,1,64,128]{3,2,1,0:T(8,128)S(1)} %get-tuple-element.17), channel_id=1, source_target_pairs={{0,2},{2,4},{4,6},{1,3},{3,5},{5,7},{8,10},{10,12},{12,14},{9,11},... | collective-permute-start | bytes 589832 | tf_op jit(solution)/shard_map/ppermute | solution.py:14
  163.7 8.5 %collective-permute-start.9 = (f32[6,1,64,128]{3,2,1,0:T(8,128)S(1)}, f32[6,1,64,128]{3,2,1,0:T(8,128)S(1)}, u32[]{:S(2)}, u32[]{:S(2)}) collective-permute-start(f32[6,1,64,128]{3,2,1,0:T(8,128)S(1)} %get-tuple-element.18), channel_id=1, source_target_pairs={{2,0},{4,2},{6,4},{3,1},{5,3},{7,5},{10,8},{12,10},{14,12},{11,9},... | collective-permute-start | bytes 589832 | tf_op jit(solution)/shard_map/ppermute | solution.py:17
  172.5 4.6 %collective-permute-start.11 = (f32[6,66,1,128]{3,1,2,0:T(8,128)S(1)}, f32[6,66,1,128]{3,1,2,0:T(8,128)S(1)}, u32[]{:S(2)}, u32[]{:S(2)}) collective-permute-start(f32[6,66,1,128]{3,1,2,0:T(8,128)S(1)} %copy.24), channel_id=1, source_target_pairs={{1,0},{3,2},{5,4},{7,6},{9,8},{11,10},{13,12},{15,14},{17,16},{19,... | collective-permute-start | bytes 608264 | tf_op jit(solution)/shard_map/ppermute | solution.py:17
  173.9 4.1 %collective-permute-start.10 = (f32[6,66,1,128]{3,1,2,0:T(8,128)S(1)}, f32[6,66,1,128]{3,1,2,0:T(8,128)S(1)}, u32[]{:S(2)}, u32[]{:S(2)}) collective-permute-start(f32[6,66,1,128]{3,1,2,0:T(8,128)S(1)} %copy.22), channel_id=1, source_target_pairs={{0,1},{2,3},{4,5},{6,7},{8,9},{10,11},{12,13},{14,15},{16,17},{18,... | collective-permute-start | bytes 608264 | tf_op jit(solution)/shard_map/ppermute | solution.py:14
  207.1 56.0 %copy-start.1 = (f32[4,64,64,128]{3,2,1,0:T(8,128)S(1)}, f32[4,64,64,128]{3,2,1,0:T(8,128)}, u32[]{:S(2)}) copy-start(f32[4,64,64,128]{3,2,1,0:T(8,128)} %fusion.19) | copy-start | bytes 25165828
  209.8 49.0 %collective-permute-start.12 = (f32[1,64,64,128]{3,2,1,0:T(8,128)S(1)}, f32[1,64,64,128]{3,2,1,0:T(8,128)S(1)}, u32[]{:S(2)}, u32[]{:S(2)}) collective-permute-start(f32[1,64,64,128]{3,2,1,0:T(8,128)S(1)} %get-tuple-element.23), channel_id=1, source_target_pairs={{0,8},{8,16},{16,24},{1,9},{9,17},{17,25},{2,10},{10,18},{18,26},{... | collective-permute-start | bytes 6291464 | tf_op jit(solution)/shard_map/ppermute | solution.py:14
  213.6 49.5 %collective-permute-start.13 = (f32[1,64,64,128]{3,2,1,0:T(8,128)S(1)}, f32[1,64,64,128]{3,2,1,0:T(8,128)S(1)}, u32[]{:S(2)}, u32[]{:S(2)}) collective-permute-start(f32[1,64,64,128]{3,2,1,0:T(8,128)S(1)} %get-tuple-element.24), channel_id=1, source_target_pairs={{8,0},{16,8},{24,16},{9,1},{17,9},{25,17},{10,2},{18,10},{26,18},{... | collective-permute-start | bytes 6291464 | tf_op jit(solution)/shard_map/ppermute | solution.py:17
  263.1 11.1 %copy-start.6 = (f32[1,64,64,128]{3,2,1,0:T(8,128)}, f32[1,64,64,128]{3,2,1,0:T(8,128)S(1)}, u32[]{:S(2)}) copy-start(f32[1,64,64,128]{3,2,1,0:T(8,128)S(1)} %collective-permute-done.13) | copy-start | bytes 6291460
  263.1 5.8 %collective-permute-start.14 = (f32[6,1,64,128]{3,2,1,0:T(8,128)S(1)}, f32[6,1,64,128]{3,2,1,0:T(8,128)S(1)}, u32[]{:S(2)}, u32[]{:S(2)}) collective-permute-start(f32[6,1,64,128]{3,2,1,0:T(8,128)S(1)} %get-tuple-element.15), channel_id=1, source_target_pairs={{0,2},{2,4},{4,6},{1,3},{3,5},{5,7},{8,10},{10,12},{12,14},{9,11},... | collective-permute-start | bytes 589832 | tf_op jit(solution)/shard_map/ppermute | solution.py:14
  265.4 8.5 %collective-permute-start.15 = (f32[6,1,64,128]{3,2,1,0:T(8,128)S(1)}, f32[6,1,64,128]{3,2,1,0:T(8,128)S(1)}, u32[]{:S(2)}, u32[]{:S(2)}) collective-permute-start(f32[6,1,64,128]{3,2,1,0:T(8,128)S(1)} %get-tuple-element.16), channel_id=1, source_target_pairs={{2,0},{4,2},{6,4},{3,1},{5,3},{7,5},{10,8},{12,10},{14,12},{11,9},... | collective-permute-start | bytes 589832 | tf_op jit(solution)/shard_map/ppermute | solution.py:17
  274.2 4.4 %collective-permute-start.17 = (f32[6,66,1,128]{3,1,2,0:T(8,128)S(1)}, f32[6,66,1,128]{3,1,2,0:T(8,128)S(1)}, u32[]{:S(2)}, u32[]{:S(2)}) collective-permute-start(f32[6,66,1,128]{3,1,2,0:T(8,128)S(1)} %copy.28), channel_id=1, source_target_pairs={{1,0},{3,2},{5,4},{7,6},{9,8},{11,10},{13,12},{15,14},{17,16},{19,... | collective-permute-start | bytes 608264 | tf_op jit(solution)/shard_map/ppermute | solution.py:17
  275.6 4.1 %collective-permute-start.16 = (f32[6,66,1,128]{3,1,2,0:T(8,128)S(1)}, f32[6,66,1,128]{3,1,2,0:T(8,128)S(1)}, u32[]{:S(2)}, u32[]{:S(2)}) collective-permute-start(f32[6,66,1,128]{3,1,2,0:T(8,128)S(1)} %copy.26), channel_id=1, source_target_pairs={{0,1},{2,3},{4,5},{6,7},{8,9},{10,11},{12,13},{14,15},{16,17},{18,... | collective-permute-start | bytes 608264 | tf_op jit(solution)/shard_map/ppermute | solution.py:14
  308.8 55.8 %copy-start.2 = (f32[4,64,64,128]{3,2,1,0:T(8,128)S(1)}, f32[4,64,64,128]{3,2,1,0:T(8,128)}, u32[]{:S(2)}) copy-start(f32[4,64,64,128]{3,2,1,0:T(8,128)} %fusion.11) | copy-start | bytes 25165828
  311.5 48.8 %collective-permute-start.18 = (f32[1,64,64,128]{3,2,1,0:T(8,128)S(1)}, f32[1,64,64,128]{3,2,1,0:T(8,128)S(1)}, u32[]{:S(2)}, u32[]{:S(2)}) collective-permute-start(f32[1,64,64,128]{3,2,1,0:T(8,128)S(1)} %get-tuple-element.21), channel_id=1, source_target_pairs={{0,8},{8,16},{16,24},{1,9},{9,17},{17,25},{2,10},{10,18},{18,26},{... | collective-permute-start | bytes 6291464 | tf_op jit(solution)/shard_map/ppermute | solution.py:14
  315.1 49.5 %collective-permute-start.19 = (f32[1,64,64,128]{3,2,1,0:T(8,128)S(1)}, f32[1,64,64,128]{3,2,1,0:T(8,128)S(1)}, u32[]{:S(2)}, u32[]{:S(2)}) collective-permute-start(f32[1,64,64,128]{3,2,1,0:T(8,128)S(1)} %get-tuple-element.22), channel_id=1, source_target_pairs={{8,0},{16,8},{24,16},{9,1},{17,9},{25,17},{10,2},{18,10},{26,18},{... | collective-permute-start | bytes 6291464 | tf_op jit(solution)/shard_map/ppermute | solution.py:17
  364.6 11.1 %copy-start.5 = (f32[1,64,64,128]{3,2,1,0:T(8,128)}, f32[1,64,64,128]{3,2,1,0:T(8,128)S(1)}, u32[]{:S(2)}) copy-start(f32[1,64,64,128]{3,2,1,0:T(8,128)S(1)} %collective-permute-done.19) | copy-start | bytes 6291460
  364.7 5.8 %collective-permute-start.20 = (f32[6,1,64,128]{3,2,1,0:T(8,128)S(1)}, f32[6,1,64,128]{3,2,1,0:T(8,128)S(1)}, u32[]{:S(2)}, u32[]{:S(2)}) collective-permute-start(f32[6,1,64,128]{3,2,1,0:T(8,128)S(1)} %get-tuple-element.13), channel_id=1, source_target_pairs={{0,2},{2,4},{4,6},{1,3},{3,5},{5,7},{8,10},{10,12},{12,14},{9,11},... | collective-permute-start | bytes 589832 | tf_op jit(solution)/shard_map/ppermute | solution.py:14
  366.9 8.5 %collective-permute-start.21 = (f32[6,1,64,128]{3,2,1,0:T(8,128)S(1)}, f32[6,1,64,128]{3,2,1,0:T(8,128)S(1)}, u32[]{:S(2)}, u32[]{:S(2)}) collective-permute-start(f32[6,1,64,128]{3,2,1,0:T(8,128)S(1)} %get-tuple-element.14), channel_id=1, source_target_pairs={{2,0},{4,2},{6,4},{3,1},{5,3},{7,5},{10,8},{12,10},{14,12},{11,9},... | collective-permute-start | bytes 589832 | tf_op jit(solution)/shard_map/ppermute | solution.py:17
  375.8 4.6 %collective-permute-start.23 = (f32[6,66,1,128]{3,1,2,0:T(8,128)S(1)}, f32[6,66,1,128]{3,1,2,0:T(8,128)S(1)}, u32[]{:S(2)}, u32[]{:S(2)}) collective-permute-start(f32[6,66,1,128]{3,1,2,0:T(8,128)S(1)} %copy.32), channel_id=1, source_target_pairs={{1,0},{3,2},{5,4},{7,6},{9,8},{11,10},{13,12},{15,14},{17,16},{19,... | collective-permute-start | bytes 608264 | tf_op jit(solution)/shard_map/ppermute | solution.py:17
  377.1 4.1 %collective-permute-start.22 = (f32[6,66,1,128]{3,1,2,0:T(8,128)S(1)}, f32[6,66,1,128]{3,1,2,0:T(8,128)S(1)}, u32[]{:S(2)}, u32[]{:S(2)}) collective-permute-start(f32[6,66,1,128]{3,1,2,0:T(8,128)S(1)} %copy.30), channel_id=1, source_target_pairs={{0,1},{2,3},{4,5},{6,7},{8,9},{10,11},{12,13},{14,15},{16,17},{18,... | collective-permute-start | bytes 608264 | tf_op jit(solution)/shard_map/ppermute | solution.py:14
where the time goes:
time: 411 us; the launch traced here: 410 us
  waiting for transfers between devices  222 us (54%)
  other arithmetic  115 us (28%)
  starting transfers between devices  55.5 us (14%)
  local copies, waits for them, and re-layouts  16.8 us (4%)
    ppermute x12, waiting for transfers between devices, extended(): lax.ppermute(lax.slice_in_dim(block, block.shape[dim] - width, None, axis...  187 us
    add x4, other arithmetic, advance(): return 2.0 * middle - before + speed_square * spread  114 us
    ppermute x12, starting transfers between devices, extended(): lax.ppermute(lax.slice_in_dim(block, block.shape[dim] - width, None, axis...  40 us
    ppermute x12, waiting for transfers between devices, extended(): lax.ppermute(lax.slice_in_dim(block, 0, width, axis=dim), axis, backward)  35.1 us
    ppermute x12, starting transfers between devices, extended(): lax.ppermute(lax.slice_in_dim(block, 0, width, axis=dim), axis, backward)  15.5 us
  transfers between devices with their start and end apart: 24, of which 20 were waited for; matrix products, arithmetic and copies ran while one was open for 1% of the time, Pallas kernels for 0%

commit v1 on v0

v1 whole, which is shorter than its diff:
```python
import functools
import math

import jax
import jax.numpy as jnp
from jax import lax
from jax.experimental import pallas as pl
from jax.experimental.pallas import tpu as pltpu
from jax.sharding import PartitionSpec as P

STEPS = 4
CHUNKS = 8
PAD = 8
AXES = ("lat", "lon", "lev")
MESH = pl.DeviceIdType.MESH


def kernel(
    counts,
    chunks,
    start_ref,
    earlier_ref,
    speed_ref,
    end_ref,
    even,
    odd,
    speed,
    load_sem,
    lat_send,
    lat_recv,
    side_send,
    side_recv,
):
    rows, columns, depth, lanes = start_ref.shape
    width = columns // chunks
    fields = (even, odd)
    me = [lax.axis_index(axis) for axis in AXES]
    inside = pl.ds(PAD, depth)
    below = [place > 0 for place in me]
    above = [place < count - 1 for place, count in zip(me, counts)]
    has = [(below[dim], above[dim]) for dim in range(3)]

    loads = [
        pltpu.make_async_copy(start_ref, even.at[pl.ds(1, rows), pl.ds(1, columns), inside], load_sem.at[0]),
        pltpu.make_async_copy(earlier_ref, odd.at[pl.ds(1, rows), pl.ds(1, columns), inside], load_sem.at[1]),
        pltpu.make_async_copy(speed_ref, speed, load_sem.at[2]),
    ]

    barrier = pltpu.get_barrier_semaphore()
    greeted = jnp.int32(0)
    for dim, axis in enumerate(AXES):
        for side, shift in enumerate((-1, 1)):
            greeted = greeted + has[dim][side].astype(jnp.int32)

            @pl.when(has[dim][side])
            def _():
                pl.semaphore_signal(barrier, inc=1, device_id={axis: me[dim] + shift}, device_id_type=MESH)

    pl.semaphore_wait(barrier, greeted)

    def lat_copy(step, side, chunk, target):
        field = fields[step % 2]
        first = chunk * width
        if step == 0:
            source = start_ref.at[(0, rows - 1)[side], pl.ds(first, width)]
        else:
            source = field.at[(1, rows)[side], pl.ds(first + 1, width), inside]
        return pltpu.make_async_remote_copy(
            src_ref=source,
            dst_ref=field.at[(rows + 1, 0)[side], pl.ds(first + 1, width), inside],
            send_sem=lat_send.at[step % 2, side, chunk],
            recv_sem=lat_recv.at[step % 2, side, chunk],
            device_id={"lat": target},
            device_id_type=MESH,
        )

    def side_copy(step, dim, side, target):
        field = fields[step % 2]
        if dim == 1:
            if step == 0:
                source = start_ref.at[:, (0, columns - 1)[side]]
            else:
                source = field.at[pl.ds(1, rows), (1, columns)[side], inside]
            dest = field.at[pl.ds(1, rows), (columns + 1, 0)[side], inside]
        else:
            if step == 0:
                source = start_ref.at[:, :, pl.ds((0, depth - PAD)[side], PAD)]
            else:
                source = field.at[pl.ds(1, rows), pl.ds(1, columns), pl.ds((PAD, depth)[side], PAD)]
            dest = field.at[pl.ds(1, rows), pl.ds(1, columns), pl.ds((PAD + depth, 0)[side], PAD)]
        return pltpu.make_async_remote_copy(
            src_ref=source,
            dst_ref=dest,
            send_sem=side_send.at[step % 2, dim - 1, side],
            recv_sem=side_recv.at[step % 2, dim - 1, side],
            device_id={AXES[dim]: target},
            device_id_type=MESH,
        )

    def lat_each(step, chunk, act):
        for side, shift in enumerate((-1, 1)):
            incoming = act == "recv"

            @pl.when(has[0][1 - side if incoming else side])
            def _():
                copy = lat_copy(step, side, chunk, me[0] - shift if incoming else me[0] + shift)
                if incoming:
                    copy.wait_recv()
                elif act == "send":
                    copy.wait_send()
                else:
                    copy.start()

    def side_each(step, act):
        for dim in (1, 2):
            for side, shift in enumerate((-1, 1)):
                incoming = act == "recv"

                @pl.when(has[dim][1 - side if incoming else side])
                def _():
                    copy = side_copy(step, dim, side, me[dim] - shift if incoming else me[dim] + shift)
                    if incoming:
                        copy.wait_recv()
                    elif act == "send":
                        copy.wait_send()
                    else:
                        copy.start()

    @pl.loop(0, chunks)
    def _(chunk):
        lat_each(0, chunk, "start")

    side_each(0, "start")
    for load in loads:
        load.start()

    for side in (0, 1):

        @pl.when(jnp.logical_not(has[0][side]))
        def _():
            @pl.loop(1, columns + 1)
            def _(x):
                for field in fields:
                    field[(0, rows + 1)[side], x, inside] = jnp.zeros((depth, lanes), jnp.float32)

        @pl.when(jnp.logical_not(has[1][side]))
        def _():
            for field in fields:
                for y in range(1, rows + 1):
                    field[y, (0, columns + 1)[side], inside] = jnp.zeros((depth, lanes), jnp.float32)

        @pl.when(jnp.logical_not(has[2][side]))
        def _():
            @pl.loop(1, columns + 1)
            def _(x):
                for field in fields:
                    for y in range(1, rows + 1):
                        field[y, x, pl.ds((0, PAD + depth)[side], PAD)] = jnp.zeros((PAD, lanes), jnp.float32)

    for load in loads:
        load.wait()

    outer = (1, rows) if rows > 1 else (1,)
    inner = tuple(range(2, rows))

    for step in range(STEPS):
        now, other = fields[step % 2], fields[(step + 1) % 2]
        last = step == STEPS - 1
        side_each(step, "recv")
        if step > 0:
            side_each(step - 1, "send")

        def advance(y, x):
            middle = now[y, x, inside]
            spread = (
                now[y - 1, x, inside]
                + now[y + 1, x, inside]
                + now[y, x - 1, inside]
                + now[y, x + 1, inside]
                + now[y, x, pl.ds(PAD - 1, depth)]
                + now[y, x, pl.ds(PAD + 1, depth)]
                - 6.0 * middle
            )
            later = 2.0 * middle - other[y, x, inside] + speed[y - 1, x - 1] * spread
            if last:
                end_ref[y - 1, x - 1] = later
            else:
                other[y, x, inside] = later

        @pl.loop(0, chunks)
        def _(chunk):
            lat_each(step, chunk, "recv")
            if step > 0:
                lat_each(step - 1, chunk, "send")
            for planes in (outer, inner):
                if planes:

                    @pl.loop(0, width)
                    def _(offset):
                        for y in planes:
                            advance(y, chunk * width + offset + 1)

            if not last:
                lat_each(step + 1, chunk, "start")

        if not last:
            side_each(step + 1, "start")

    side_each(STEPS - 1, "send")

    @pl.loop(0, chunks)
    def _(chunk):
        lat_each(STEPS - 1, chunk, "send")


def solution(mesh):
    counts = tuple(mesh.shape[axis] for axis in AXES)

    def shards(pressure, earlier, speed_square):
        rows, columns, depth, lanes = pressure.shape
        chunks = math.gcd(columns, CHUNKS)
        field = pltpu.VMEM((rows + 2, columns + 2, depth + 2 * PAD, lanes), jnp.float32)
        return pl.pallas_call(
            functools.partial(kernel, counts, chunks),
            out_shape=pltpu.VMEM(pressure.shape, jnp.float32),
            in_specs=[pl.BlockSpec(memory_space=pltpu.HBM)] * 3,
            out_specs=pl.BlockSpec(memory_space=pltpu.VMEM),
            scratch_shapes=[
                field,
                field,
                pltpu.VMEM(pressure.shape, jnp.float32),
                pltpu.SemaphoreType.DMA((3,)),
                pltpu.SemaphoreType.DMA((2, 2, chunks)),
                pltpu.SemaphoreType.DMA((2, 2, chunks)),
                pltpu.SemaphoreType.DMA((2, 2, 2)),
                pltpu.SemaphoreType.DMA((2, 2, 2)),
            ],
            compiler_params=pltpu.CompilerParams(
                collective_id=0, has_side_effects=True, vmem_limit_bytes=44 * 2**20
            ),
        )(pressure, earlier, speed_square)

    spec = P("lat", "lon", "lev", None)
    return jax.shard_map(
        shards, mesh=mesh, in_specs=(spec, spec, spec), out_specs=spec, check_vma=False
    )
```

time: 411 us -> 190 us (0.46)
  waiting for transfers between devices: 222 us -> 0 us
  Pallas kernels: 0 us -> 186 us
  other arithmetic: 115 us -> 0 us
  starting transfers between devices: 55.5 us -> 0 us
  local copies, waits for them, and re-layouts: 16.8 us -> 3.4 us
    ppermute x24 -> x0, waiting for transfers between devices: 222 us -> none  [the longest x12 187 us: extended(): lax.ppermute(lax.slice_in_dim(block, block.shape[dim] - width, None, axis...]
    pallas_call x0 -> x1, Pallas kernels: none -> 186 us  [shards(): pl.pallas_call(functools.partial(kernel, counts, chunks), out_shape=pltpu...]
    add x4 -> x0, other arithmetic: 114 us -> none  [advance(): return 2.0 * middle - before + speed_square * spread]
    ppermute x24 -> x0, starting transfers between devices: 55.5 us -> none  [the longest x12 40 us: extended(): lax.ppermute(lax.slice_in_dim(block, block.shape[dim] - width, None, axis...]
    slice x13 -> x0, local copies, waits for them, and re-layouts: 10.2 us -> none  [the longest x8 6 us: extended(): lax.slice_in_dim(block, block.shape[dim] - width, None, axis=dim)]
  transfers between devices with their start and end apart: 24 -> 0, of which waited for: 20 -> 0; matrix products, arithmetic and copies ran while one was open for 1% -> 0% of each run, Pallas kernels for 0% -> 0%
where the time goes in v1:
time: 190 us
  Pallas kernels  186 us (98%)
  local copies, waits for them, and re-layouts  3.4 us (2%)
    pallas_call x1, Pallas kernels, shards(): pl.pallas_call(functools.partial(kernel, counts, chunks), out_shape=pltpu...  186 us

profile of v1, /device:TPU:0, one launch (start us, length us, event | category | flops | bytes accessed | tf_op | source)
XLA Modules:
  0.0 189.8 jit_solution(8102624632826496482)
XLA Ops:
  0.0 186.3 %shard_map.37 = f32[4,64,64,128]{3,2,1,0:T(8,128)S(1)} custom-call(f32[4,64,64,128]{3,2,1,0:T(8,128)} %start_ref.1, f32[4,64,64,128]{3,2,1,0:T(8,128)} %earlier_ref.1, f32[4,64,64,128]{3,2,1,0:T(8,128)} %speed_ref.1), custom_call_target="tpu_custom_call" | custom-call | tf_op jit(solution)/shard_map/pallas_call | solution.py:223
  186.4 3.4 %copy.5 = f32[4,64,64,128]{3,2,1,0:T(8,128)} copy(f32[4,64,64,128]{3,2,1,0:T(8,128)S(1)} %shard_map.37) | data formatting | bytes 16777216

commit v2 on v1

--- a/solution.py
+++ b/solution.py
@@ -9,7 +9,7 @@
 from jax.sharding import PartitionSpec as P
 
 STEPS = 4
-CHUNKS = 8
+CHUNKS = 16
 PAD = 8
 AXES = ("lat", "lon", "lev")
 MESH = pl.DeviceIdType.MESH
@@ -40,11 +40,36 @@
     above = [place < count - 1 for place, count in zip(me, counts)]
     has = [(below[dim], above[dim]) for dim in range(3)]
 
+    edges = (0, rows - 1) if rows > 1 else (0,)
+    early = [
+        pltpu.make_async_copy(
+            start_ref.at[plane, pl.ds(0, width)], even.at[plane + 1, pl.ds(1, width), inside], load_sem.at[place]
+        )
+        for place, plane in enumerate(edges)
+    ]
     loads = [
-        pltpu.make_async_copy(start_ref, even.at[pl.ds(1, rows), pl.ds(1, columns), inside], load_sem.at[0]),
-        pltpu.make_async_copy(earlier_ref, odd.at[pl.ds(1, rows), pl.ds(1, columns), inside], load_sem.at[1]),
-        pltpu.make_async_copy(speed_ref, speed, load_sem.at[2]),
+        pltpu.make_async_copy(earlier_ref, odd.at[pl.ds(1, rows), pl.ds(1, columns), inside], load_sem.at[2]),
+        pltpu.make_async_copy(speed_ref, speed, load_sem.at[3]),
     ]
+    if chunks > 1:
+        loads += [
+            pltpu.make_async_copy(
+                start_ref.at[plane, pl.ds(width, columns - width)],
+                even.at[plane + 1, pl.ds(1 + width, columns - width), inside],
+                load_sem.at[4 + place],
+            )
+            for place, plane in enumerate(edges)
+        ]
+    if rows > 2:
+        loads.append(
+            pltpu.make_async_copy(
+                start_ref.at[pl.ds(1, rows - 2)],
+                even.at[pl.ds(2, rows - 2), pl.ds(1, columns), inside],
+                load_sem.at[6],
+            )
+        )
+    for load in early:
+        load.start()
 
     barrier = pltpu.get_barrier_semaphore()
     greeted = jnp.int32(0)
@@ -58,10 +83,10 @@
 
     pl.semaphore_wait(barrier, greeted)
 
-    def lat_copy(step, side, chunk, target):
+    def lat_copy(step, side, chunk, target, held):
         field = fields[step % 2]
         first = chunk * width
-        if step == 0:
+        if step == 0 and not held:
             source = start_ref.at[(0, rows - 1)[side], pl.ds(first, width)]
         else:
             source = field.at[(1, rows)[side], pl.ds(first + 1, width), inside]
@@ -97,13 +122,13 @@
             device_id_type=MESH,
         )
 
-    def lat_each(step, chunk, act):
+    def lat_each(step, chunk, act, held=False):
         for side, shift in enumerate((-1, 1)):
             incoming = act == "recv"
 
             @pl.when(has[0][1 - side if incoming else side])
             def _():
-                copy = lat_copy(step, side, chunk, me[0] - shift if incoming else me[0] + shift)
+                copy = lat_copy(step, side, chunk, me[0] - shift if incoming else me[0] + shift, held)
                 if incoming:
                     copy.wait_recv()
                 elif act == "send":
@@ -126,7 +151,11 @@
                     else:
                         copy.start()
 
-    @pl.loop(0, chunks)
+    for load in early:
+        load.wait()
+    lat_each(0, 0, "start", held=True)
+
+    @pl.loop(1, chunks)
     def _(chunk):
         lat_each(0, chunk, "start")
 
@@ -189,10 +218,7 @@
 
         @pl.loop(0, chunks)
         def _(chunk):
-            lat_each(step, chunk, "recv")
-            if step > 0:
-                lat_each(step - 1, chunk, "send")
-            for planes in (outer, inner):
+            def compute(planes):
                 if planes:
 
                     @pl.loop(0, width)
@@ -200,6 +226,14 @@
                         for y in planes:
                             advance(y, chunk * width + offset + 1)
 
+            if last:
+                compute(inner)
+            lat_each(step, chunk, "recv")
+            if step > 0:
+                lat_each(step - 1, chunk, "send")
+            compute(outer)
+            if not last:
+                compute(inner)
             if not last:
                 lat_each(step + 1, chunk, "start")
 
@@ -229,7 +263,7 @@
                 field,
                 field,
                 pltpu.VMEM(pressure.shape, jnp.float32),
-                pltpu.SemaphoreType.DMA((3,)),
+                pltpu.SemaphoreType.DMA((7,)),
                 pltpu.SemaphoreType.DMA((2, 2, chunks)),
                 pltpu.SemaphoreType.DMA((2, 2, chunks)),
                 pltpu.SemaphoreType.DMA((2, 2, 2)),

time: 190 us -> 190 us (level)
  no operation moved by 1% of the time
where the time goes in v2:
time: 190 us
  Pallas kernels  186 us (98%)
  local copies, waits for them, and re-layouts  3.4 us (2%)
    pallas_call x1, Pallas kernels, shards(): pl.pallas_call(functools.partial(kernel, counts, chunks), out_shape=pltpu...  186 us

profile of v2, /device:TPU:0, one launch (start us, length us, event | category | flops | bytes accessed | tf_op | source)
XLA Modules:
  0.0 189.8 jit_solution(12227837200437011787)
XLA Ops:
  0.0 186.4 %shard_map.37 = f32[4,64,64,128]{3,2,1,0:T(8,128)S(1)} custom-call(f32[4,64,64,128]{3,2,1,0:T(8,128)} %start_ref.1, f32[4,64,64,128]{3,2,1,0:T(8,128)} %earlier_ref.1, f32[4,64,64,128]{3,2,1,0:T(8,128)} %speed_ref.1), custom_call_target="tpu_custom_call" | custom-call | tf_op jit(solution)/shard_map/pallas_call | solution.py:257
  186.4 3.4 %copy.5 = f32[4,64,64,128]{3,2,1,0:T(8,128)} copy(f32[4,64,64,128]{3,2,1,0:T(8,128)S(1)} %shard_map.37) | data formatting | bytes 16777216

commit v3 on v2

--- a/solution.py
+++ b/solution.py
@@ -9,7 +9,7 @@
 from jax.sharding import PartitionSpec as P
 
 STEPS = 4
-CHUNKS = 16
+CHUNKS = 8
 PAD = 8
 AXES = ("lat", "lon", "lev")
 MESH = pl.DeviceIdType.MESH

time: 190 us -> 189 us (level)
  no operation moved by 1% of the time
where the time goes in v3:
time: 189 us
  Pallas kernels  186 us (98%)
  local copies, waits for them, and re-layouts  3.4 us (2%)
    pallas_call x1, Pallas kernels, shards(): pl.pallas_call(functools.partial(kernel, counts, chunks), out_shape=pltpu...  186 us

profile of v3, /device:TPU:0, one launch (start us, length us, event | category | flops | bytes accessed | tf_op | source)
XLA Modules:
  0.0 189.3 jit_solution(2024635173975481522)
XLA Ops:
  0.0 185.9 %shard_map.37 = f32[4,64,64,128]{3,2,1,0:T(8,128)S(1)} custom-call(f32[4,64,64,128]{3,2,1,0:T(8,128)} %start_ref.1, f32[4,64,64,128]{3,2,1,0:T(8,128)} %earlier_ref.1, f32[4,64,64,128]{3,2,1,0:T(8,128)} %speed_ref.1), custom_call_target="tpu_custom_call" | custom-call | tf_op jit(solution)/shard_map/pallas_call | solution.py:257
  185.9 3.4 %copy.5 = f32[4,64,64,128]{3,2,1,0:T(8,128)} copy(f32[4,64,64,128]{3,2,1,0:T(8,128)S(1)} %shard_map.37) | data formatting | bytes 16777216
